TPU v7x, 512 devices: a whole 4x4x16 slice. The times are simulated.
512 devices in a mesh: dp: 16 (over z_lo, core), block: 32 (over y, z_hi, x).
Axes of the slice: x: 4, y: 4, z: 16 (z_hi: 2, z_lo: 8; z = z_hi * 8 + z_lo), core: 2. Of those that a mesh axis runs over, the one named last changes fastest.
Arguments:
- tokens: bfloat16 [4096, 16384], P('dp', 'block'), may hold values from -6 to 6
- upper_left: bfloat16 [64, 256, 1024], P('block', 'dp'), may hold values from -0.375 to 0.375
- upper_right: bfloat16 [256, 256, 256], P('block', 'dp'), may hold values from -0.375 to 0.375
- lower_right: bfloat16 [256, 256, 256], P('block', 'dp'), may hold values from -0.375 to 0.375
- lower_left: bfloat16 [64, 1024, 256], P('block', 'dp'), may hold values from -0.1875 to 0.1875
- cotangent: bfloat16 [4096, 16384], P('dp', 'block'), may hold values from -6 to 6
Outputs:
- output: bfloat16 [4096, 16384], P('dp', 'block')
- token_grad: bfloat16 [4096, 16384], P('dp', 'block')
- upper_left_grad: float32 [64, 256, 1024], P('block', 'dp')
- upper_right_grad: float32 [256, 256, 256], P('block', 'dp')
- lower_right_grad: float32 [256, 256, 256], P('block', 'dp')
- lower_left_grad: float32 [64, 1024, 256], P('block', 'dp')
All inputs are finite; a program needn't handle non-finite values.
Results may differ from a plain program's by a relative error of at most 0.017.
Values may be sent and summed in bfloat16 or wider, within the bound.
A program may use at most 64 MiB of HBM per device.

v0:
```python
import jax
import jax.numpy as jnp
from jax import lax
from jax.sharding import PartitionSpec as P


def contract(form, left, right):
    return jnp.einsum(form, left, right, preferred_element_type=jnp.float32)


def permute(values):
    return lax.all_to_all(values, "block", split_axis=1, concat_axis=0, tiled=True)


def forward(tokens, weights, mover):
    in_left, in_right, out_right, out_left = weights
    width = in_right.shape[1]
    rows = tokens.shape[0]
    local_blocks = in_left.shape[0]
    expand = in_left.shape[2] // width
    x_three = tokens.reshape(rows, local_blocks, width)
    left_four = in_left.reshape(local_blocks, width, expand, width)
    mixed = (
        contract("tkb,kbec->kect", x_three, left_four)
        .astype(jnp.bfloat16)
        .reshape(local_blocks * expand, width, rows)
    )
    spread = mover(mixed)
    hidden_pre = contract("act,cab->cbt", spread, in_right)
    active = jax.nn.gelu(hidden_pre).astype(jnp.bfloat16)
    narrow = contract("cbt,cbe->cet", active, out_right).astype(jnp.bfloat16)
    gathered = mover(narrow)
    narrow_four = gathered.reshape(width, local_blocks, expand, rows)
    out_four = out_left.reshape(local_blocks, expand, width, width)
    result = (
        contract("ckft,kfco->tko", narrow_four, out_four)
        .astype(jnp.bfloat16)
        .reshape(rows, local_blocks * width)
    )
    return (result, spread, hidden_pre, active, narrow_four)


def local(tokens, upper_left, upper_right, lower_right, lower_left, cotangent):
    weights = (
        lax.all_gather(upper_left, "dp", axis=1, tiled=True),
        lax.all_gather(upper_right, "dp", axis=1, tiled=True),
        lax.all_gather(lower_right, "dp", axis=1, tiled=True),
        lax.all_gather(lower_left, "dp", axis=1, tiled=True),
    )
    in_left, in_right, out_right, out_left = weights
    width = in_right.shape[1]
    rows = tokens.shape[0]
    local_blocks = in_left.shape[0]
    expand = in_left.shape[2] // width
    result, spread, hidden_pre, active, narrow_four = forward(tokens, weights, permute)
    x_three = tokens.reshape(rows, local_blocks, width)
    left_four = in_left.reshape(local_blocks, width, expand, width)
    out_four = out_left.reshape(local_blocks, expand, width, width)
    cot_three = cotangent.reshape(rows, local_blocks, width)
    grad_lower_left = contract("ckft,tko->kfco", narrow_four, cot_three).reshape(
        local_blocks, expand * width, width
    )
    back_narrow = (
        contract("tko,kfco->kfct", cot_three, out_four)
        .astype(jnp.bfloat16)
        .reshape(local_blocks * expand, width, rows)
    )
    narrow_back = permute(back_narrow)
    grad_lower_right = contract("cbt,ect->cbe", active, narrow_back)
    back_active = contract("ect,cbe->cbt", narrow_back, out_right)
    back_pre = jax.vjp(jax.nn.gelu, hidden_pre)[1](back_active)[0].astype(jnp.bfloat16)
    grad_upper_right = contract("act,cbt->cab", spread, back_pre)
    back_mixed = contract("cbt,cab->cat", back_pre, in_right).astype(jnp.bfloat16)
    mixed_back = permute(back_mixed).reshape(width, local_blocks, expand, rows)
    grad_upper_left = contract("tkb,cket->kbec", x_three, mixed_back).reshape(
        local_blocks, width, expand * width
    )
    token_grad = (
        contract("cket,kbec->tkb", mixed_back, left_four)
        .astype(jnp.bfloat16)
        .reshape(rows, local_blocks * width)
    )
    grad_upper_left, grad_upper_right, grad_lower_right, grad_lower_left = (
        lax.psum_scatter(
            grad_upper_left.astype(jnp.bfloat16), "dp", scatter_dimension=1, tiled=True
        ).astype(jnp.float32),
        lax.psum_scatter(
            grad_upper_right.astype(jnp.bfloat16), "dp", scatter_dimension=1, tiled=True
        ).astype(jnp.float32),
        lax.psum_scatter(
            grad_lower_right.astype(jnp.bfloat16), "dp", scatter_dimension=1, tiled=True
        ).astype(jnp.float32),
        lax.psum_scatter(
            grad_lower_left.astype(jnp.bfloat16), "dp", scatter_dimension=1, tiled=True
        ).astype(jnp.float32),
    )
    return (
        result,
        token_grad,
        grad_upper_left,
        grad_upper_right,
        grad_lower_right,
        grad_lower_left,
    )


def solution(mesh):
    in_specs = (
        P("dp", "block"),
        P("block", "dp", None),
        P("block", "dp", None),
        P("block", "dp", None),
        P("block", "dp", None),
        P("dp", "block"),
    )
    out_specs = (
        P("dp", "block"),
        P("dp", "block"),
        P("block", "dp", None),
        P("block", "dp", None),
        P("block", "dp", None),
        P("block", "dp", None),
    )
    return jax.shard_map(local, mesh=mesh, in_specs=in_specs, out_specs=out_specs, check_vma=False)
```

profile of v0, /device:TPU:6, one launch (start us, length us, event | category | flops | bytes accessed | tf_op | source)
XLA Modules:
  0.0 939.5 jit_solution(8600866587322765931)
XLA Ops:
  7.2 0.0 all-gather.5.cloned.1.call-start
  7.2 0.7 all-gather.5.cloned.1.call-update
  7.9 1.0 reshape.52
  8.9 104.0 %all-gather.5.cloned.1.call-done = bf16[2,256,1024]{2,1,0:T(8,128)(2,1)} async-done(((bf16[2,16,1024]{2,1,0:T(8,128)(2,1)}), bf16[2,256,1024]{2,1,0:T(8,128)(2,1)}) %all-gather.5.cloned.1.call-update) | async-done | bytes 1048592 | tf_op jit(solution)/shard_map/all_gather | solution.py:45
  112.9 1.5 copy.72
  114.4 0.5 convolution_convert_fusion.7
  114.8 0.0 copy-start.5
  114.8 1.6 copy.74
  116.4 18.3 %all-to-all-start = ((bf16[8,256,256]{2,0,1:T(8,128)(2,1)}), bf16[8,256,256]{2,0,1:T(8,128)(2,1)S(1)}, u32[]{:S(2)}, u32[]{:S(2)}) async-start(bf16[8,256,256]{2,0,1:T(8,128)(2,1)} %copy.74), calls=%async_computation | async-start | bytes 2097152 | tf_op jit(solution)/shard_map/all_to_all | solution.py:12
  134.7 0.0 all-gather.11.cloned.1.call-start
  134.8 0.7 all-gather.11.cloned.1.call-update
  135.5 0.1 reshape.57
  135.6 0.0 copy-start.2
  135.6 102.4 %all-gather.11.cloned.1.call-done = bf16[2,1024,256]{2,1,0:T(8,128)(2,1)} async-done(((bf16[2,64,256]{2,1,0:T(8,128)(2,1)}), bf16[2,1024,256]{2,1,0:T(8,128)(2,1)}) %all-gather.11.cloned.1.call-update) | async-done | bytes 1048592 | tf_op jit(solution)/shard_map/all_gather | solution.py:48
  238.0 1.7 convolution_convert_fusion.5
  239.7 1.6 copy.83
  241.2 16.7 %all-to-all-start.2 = ((bf16[8,256,256]{2,0,1:T(8,128)(2,1)}), bf16[8,256,256]{2,0,1:T(8,128)(2,1)}, u32[]{:S(2)}, u32[]{:S(2)}) async-start(bf16[8,256,256]{2,0,1:T(8,128)(2,1)} %copy.83), calls=%async_computation.2 | async-start | bytes 2097152 | tf_op jit(solution)/shard_map/all_to_all | solution.py:12
  257.9 0.0 all-gather.7.cloned.1.call-start
  258.0 0.7 all-gather.7.cloned.1.call-update
  258.7 0.0 all-gather.9.cloned.1.call-start
  258.7 0.5 all-gather.9.cloned.1.call-update
  259.2 0.3 copy.76
  259.6 26.5 %all-to-all-done.2 = bf16[8,256,256]{2,0,1:T(8,128)(2,1)} async-done(((bf16[8,256,256]{2,0,1:T(8,128)(2,1)}), bf16[8,256,256]{2,0,1:T(8,128)(2,1)}, u32[]{:S(2)}, u32[]{:S(2)}) %all-to-all-start.2) | async-done | bytes 1048608 | tf_op jit(solution)/shard_map/all_to_all | solution.py:12
  286.0 2.5 copy.85
  288.6 72.4 %all-gather.7.cloned.1.call-done = bf16[8,256,256]{2,1,0:T(8,128)(2,1)} async-done(((bf16[8,16,256]{2,1,0:T(8,128)(2,1)}), bf16[8,256,256]{2,1,0:T(8,128)(2,1)}) %all-gather.7.cloned.1.call-update) | async-done | bytes 1048592 | tf_op jit(solution)/shard_map/all_gather | solution.py:46
  361.0 3.1 fusion.17
  364.1 97.4 %all-gather.9.cloned.1.call-done = bf16[8,256,256]{2,1,0:T(8,128)(2,1)} async-done(((bf16[8,16,256]{2,1,0:T(8,128)(2,1)}), bf16[8,256,256]{2,1,0:T(8,128)(2,1)}) %all-gather.9.cloned.1.call-update) | async-done | bytes 1048592 | tf_op jit(solution)/shard_map/all_gather | solution.py:47
  461.5 4.0 fusion.6
  465.5 1.4 fusion.12
  467.0 2.7 copy.87
  469.7 17.5 %all-to-all-start.3 = ((bf16[8,256,256]{2,0,1:T(8,128)(2,1)}), bf16[8,256,256]{2,0,1:T(8,128)(2,1)}, u32[]{:S(2)}, u32[]{:S(2)}) async-start(bf16[8,256,256]{2,0,1:T(8,128)(2,1)} %copy.87), calls=%async_computation.3 | async-start | bytes 2097152 | tf_op jit(solution)/shard_map/all_to_all | solution.py:12
  487.2 0.0 reduce-scatter.7.cloned.1.call-start
  487.3 1.4 convolution_convert_fusion.2
  488.7 0.0 reduce-scatter.7.cloned.1.call-update
  488.7 2.7 fusion.11
  491.4 1.8 copy.78
  493.2 25.6 %all-to-all-done.3 = bf16[8,256,256]{2,0,1:T(8,128)(2,1)} async-done(((bf16[8,256,256]{2,0,1:T(8,128)(2,1)}), bf16[8,256,256]{2,0,1:T(8,128)(2,1)}, u32[]{:S(2)}, u32[]{:S(2)}) %all-to-all-start.3) | async-done | bytes 1048608 | tf_op jit(solution)/shard_map/all_to_all | solution.py:12
  518.9 21.3 %all-to-all-start.1 = ((bf16[8,256,256]{2,0,1:T(8,128)(2,1)}), bf16[8,256,256]{2,0,1:T(8,128)(2,1)S(1)}, u32[]{:S(2)}, u32[]{:S(2)}) async-start(bf16[8,256,256]{2,0,1:T(8,128)(2,1)} %copy.78), calls=%async_computation.1 | async-start | bytes 2097152 | tf_op jit(solution)/shard_map/all_to_all | solution.py:12
  540.2 0.0 reduce-scatter.9.cloned.1.call-start
  540.3 3.7 convolution_convert_fusion.1
  543.9 0.0 reduce-scatter.9.cloned.1.call-update
  544.0 0.2 reduce-scatter.5.cloned.1.call-start
  544.2 1.3 copy.89
  545.5 1.4 convolution_convert_fusion.3
  546.9 2.3 copy.92
  549.2 0.0 reduce-scatter.5.cloned.1.call-update
  549.2 0.0 reduce-scatter.11.cloned.1.call-start
  549.3 25.5 %all-to-all-done.1 = bf16[8,256,256]{2,0,1:T(8,128)(2,1)S(1)} async-done(((bf16[8,256,256]{2,0,1:T(8,128)(2,1)}), bf16[8,256,256]{2,0,1:T(8,128)(2,1)S(1)}, u32[]{:S(2)}, u32[]{:S(2)}) %all-to-all-start.1) | async-done | bytes 1048608 | tf_op jit(solution)/shard_map/all_to_all | solution.py:12
  574.8 1.0 copy-done
  575.7 1.3 copy.80
  577.0 1.4 convolution_convert_fusion
  578.4 0.0 reduce-scatter.11.cloned.1.call-update
  578.5 37.8 %reduce-scatter.7.cloned.1.call-done = bf16[8,16,256]{2,1,0:T(8,128)(2,1)} async-done(((bf16[8,256,256]{2,1,0:T(8,128)(2,1)}), bf16[8,16,256]{2,1,0:T(8,128)(2,1)}) %reduce-scatter.7.cloned.1.call-update) | async-done | bytes 65552 | tf_op jit(solution)/shard_map/reduce_scatter | solution.py:87
  616.2 1.5 convert_element_type.89
  617.8 106.2 %reduce-scatter.9.cloned.1.call-done = bf16[8,16,256]{2,1,0:T(8,128)(2,1)} async-done(((bf16[8,256,256]{2,1,0:T(8,128)(2,1)}), bf16[8,16,256]{2,1,0:T(8,128)(2,1)}) %reduce-scatter.9.cloned.1.call-update) | async-done | bytes 65552 | tf_op jit(solution)/shard_map/reduce_scatter | solution.py:90
  723.9 1.5 convert_element_type.91
  725.5 1.7 fusion.13
  727.2 0.8 copy.98
  728.0 0.5 fusion.14
  728.6 0.8 copy.99
  729.4 98.0 %reduce-scatter.5.cloned.1.call-done = bf16[2,16,1024]{2,1,0:T(8,128)(2,1)} async-done(((bf16[2,256,1024]{2,1,0:T(8,128)(2,1)}), bf16[2,16,1024]{2,1,0:T(8,128)(2,1)}) %reduce-scatter.5.cloned.1.call-update) | async-done | bytes 65552 | tf_op jit(solution)/shard_map/reduce_scatter | solution.py:84
  827.4 1.5 convert_element_type.87
  829.0 102.2 %reduce-scatter.11.cloned.1.call-done = bf16[2,64,256]{2,1,0:T(8,128)(2,1)} async-done(((bf16[2,1024,256]{2,1,0:T(8,128)(2,1)}), bf16[2,64,256]{2,1,0:T(8,128)(2,1)}) %reduce-scatter.11.cloned.1.call-update) | async-done | bytes 65552 | tf_op jit(solution)/shard_map/reduce_scatter | solution.py:93
  931.1 1.5 convert_element_type.95
  (10 shorter events, 0.0 us)
Async XLA Ops:
  7.2 105.7 %all-gather.5.cloned.1.call-start = ((), (), s32[]{:S(2)}) async-start(), calls=%async_computation.8 | async-start | bytes 1114112 | tf_op jit(solution)/shard_map/all_gather | solution.py:45
  114.8 20.7 %copy-start.5 = (bf16[256,512]{1,0:T(8,128)(2,1)S(1)}, bf16[256,512]{1,0:T(8,128)(2,1)}, u32[]{:S(2)}) copy-start(bf16[256,512]{1,0:T(8,128)(2,1)} %param.11) | copy-start | bytes 786436
  116.4 124.8 %all-to-all-start = ((bf16[8,256,256]{2,0,1:T(8,128)(2,1)}), bf16[8,256,256]{2,0,1:T(8,128)(2,1)S(1)}, u32[]{:S(2)}, u32[]{:S(2)}) async-start(bf16[8,256,256]{2,0,1:T(8,128)(2,1)} %copy.74), calls=%async_computation | async-start | bytes 2097152 | tf_op jit(solution)/shard_map/all_to_all | solution.py:12
  134.7 103.2 %all-gather.11.cloned.1.call-start = ((), (), s32[]{:S(2)}) async-start(), calls=%async_computation.11 | async-start | bytes 1114112 | tf_op jit(solution)/shard_map/all_gather | solution.py:48
  135.6 105.7 %copy-start.2 = (bf16[256,2,256]{2,1,0:T(2,128)(2,1)}, bf16[256,2,256]{2,1,0:T(2,128)(2,1)S(1)}, u32[]{:S(2)}) copy-start(bf16[256,2,256]{2,1,0:T(2,128)(2,1)S(1)} %reshape.57) | copy-start | bytes 786436
  241.2 44.8 %all-to-all-start.2 = ((bf16[8,256,256]{2,0,1:T(8,128)(2,1)}), bf16[8,256,256]{2,0,1:T(8,128)(2,1)}, u32[]{:S(2)}, u32[]{:S(2)}) async-start(bf16[8,256,256]{2,0,1:T(8,128)(2,1)} %copy.83), calls=%async_computation.2 | async-start | bytes 2097152 | tf_op jit(solution)/shard_map/all_to_all | solution.py:12
  257.9 103.1 %all-gather.7.cloned.1.call-start = ((), (), s32[]{:S(2)}) async-start(), calls=%async_computation.9 | async-start | bytes 1114112 | tf_op jit(solution)/shard_map/all_gather | solution.py:46
  258.7 202.8 %all-gather.9.cloned.1.call-start = ((), (), s32[]{:S(2)}) async-start(), calls=%async_computation.10 | async-start | bytes 1114112 | tf_op jit(solution)/shard_map/all_gather | solution.py:47
  461.5 4.0 copy-start.1
  469.7 49.2 %all-to-all-start.3 = ((bf16[8,256,256]{2,0,1:T(8,128)(2,1)}), bf16[8,256,256]{2,0,1:T(8,128)(2,1)}, u32[]{:S(2)}, u32[]{:S(2)}) async-start(bf16[8,256,256]{2,0,1:T(8,128)(2,1)} %copy.87), calls=%async_computation.3 | async-start | bytes 2097152 | tf_op jit(solution)/shard_map/all_to_all | solution.py:12
  487.2 129.0 %reduce-scatter.7.cloned.1.call-start = ((), (), s32[]{:S(2)}) async-start(), calls=%async_computation.13 | async-start | bytes 1114112 | tf_op jit(solution)/shard_map/reduce_scatter | solution.py:87
  491.4 48.8 %copy-start.4 = (bf16[32,8,8,256]{3,2,1,0:T(8,128)(2,1)S(1)}, bf16[32,8,8,256]{3,2,1,0:T(8,128)(2,1)}, u32[]{:S(2)}) copy-start(bf16[32,8,8,256]{3,2,1,0:T(8,128)(2,1)} %copy.85) | copy-start | bytes 3145732
  518.9 55.9 %all-to-all-start.1 = ((bf16[8,256,256]{2,0,1:T(8,128)(2,1)}), bf16[8,256,256]{2,0,1:T(8,128)(2,1)S(1)}, u32[]{:S(2)}, u32[]{:S(2)}) async-start(bf16[8,256,256]{2,0,1:T(8,128)(2,1)} %copy.78), calls=%async_computation.1 | async-start | bytes 2097152 | tf_op jit(solution)/shard_map/all_to_all | solution.py:12
  540.2 183.7 %reduce-scatter.9.cloned.1.call-start = ((), (), s32[]{:S(2)}) async-start(), calls=%async_computation.14 | async-start | bytes 1114112 | tf_op jit(solution)/shard_map/reduce_scatter | solution.py:90
  544.0 283.5 %reduce-scatter.5.cloned.1.call-start = ((), (), s32[]{:S(2)}) async-start(), calls=%async_computation.12 | async-start | bytes 1114112 | tf_op jit(solution)/shard_map/reduce_scatter | solution.py:84
  549.2 27.8 %copy-start.3 = (bf16[256,2,256]{2,1,0:T(2,128)(2,1)S(1)}, bf16[256,2,256]{2,1,0:T(2,128)(2,1)}, u32[]{:S(2)}) copy-start(bf16[256,2,256]{2,1,0:T(2,128)(2,1)} %copy-done.2) | copy-start | bytes 786436
  549.2 381.9 %reduce-scatter.11.cloned.1.call-start = ((), (), s32[]{:S(2)}) async-start(), calls=%async_computation.15 | async-start | bytes 1114112 | tf_op jit(solution)/shard_map/reduce_scatter | solution.py:93
  574.8 1.0 copy-start
Sparse Core Ops, SparseCore 0:
  10.1 102.7 all-gather.4
  137.6 100.2 all-gather.10
  260.8 100.1 all-gather.6
  363.0 98.5 all-gather.8
  490.5 125.6 reduce-scatter.6
  618.9 104.9 reduce-scatter.8
  726.8 100.6 reduce-scatter.4
  830.2 100.8 reduce-scatter.10
where the time goes:
time: 941 us; the launch traced here: 939 us
  waiting for transfers between devices  801 us (85%)
  starting transfers between devices  74.4 us (8%)
  matrix products  23.5 us (2%)
  local copies, waits for them, and re-layouts  20.6 us (2%)
  between operations  14.3 us (2%)
    reduce_scatter x1, waiting for transfers between devices, local(): lax.psum_scatter(grad_lower_right.astype(jnp.bfloat16), 'dp', scatter_dim...  106 us
    all_gather x1, waiting for transfers between devices, local(): lax.all_gather(upper_left, 'dp', axis=1, tiled=True)  104 us
    all_gather x1, waiting for transfers between devices, local(): lax.all_gather(lower_left, 'dp', axis=1, tiled=True)  102 us
    reduce_scatter x1, waiting for transfers between devices, local(): lax.psum_scatter(grad_lower_left.astype(jnp.bfloat16), 'dp', scatter_dime...  102 us
    reduce_scatter x1, waiting for transfers between devices, local(): lax.psum_scatter(grad_upper_left.astype(jnp.bfloat16), 'dp', scatter_dime...  98 us
    all_gather x1, waiting for transfers between devices, local(): lax.all_gather(lower_right, 'dp', axis=1, tiled=True)  97.4 us
    all_to_all x4, waiting for transfers between devices, permute(): lax.all_to_all(values, 'block', split_axis=1, concat_axis=0, tiled=True)  77.6 us
    all_to_all x4, starting transfers between devices, permute(): lax.all_to_all(values, 'block', split_axis=1, concat_axis=0, tiled=True)  73.9 us
  transfers between devices with their start and end apart: 12, of which 11 were waited for; matrix products, arithmetic and copies ran while one was open for 4% of the time, Pallas kernels for 0%

commit v1 on v0

--- a/solution.py
+++ b/solution.py
@@ -2,6 +2,10 @@
 import jax.numpy as jnp
 from jax import lax
 from jax.sharding import PartitionSpec as P
+
+supply_the_wall = lambda view: jnp.concatenate(
+    lax.all_to_all(jnp.stack(lax.axis_size("dp") * [view], axis=0), "dp", 0, 0), 1
+)
 
 
 def contract(form, left, right):
@@ -43,7 +47,7 @@
 def local(tokens, upper_left, upper_right, lower_right, lower_left, cotangent):
     weights = (
         lax.all_gather(upper_left, "dp", axis=1, tiled=True),
-        lax.all_gather(upper_right, "dp", axis=1, tiled=True),
+        supply_the_wall(upper_right),
         lax.all_gather(lower_right, "dp", axis=1, tiled=True),
         lax.all_gather(lower_left, "dp", axis=1, tiled=True),
     )

time: 941 us -> 850 us (0.903)
  waiting for transfers between devices: 801 us -> 695 us
  starting transfers between devices: 74.4 us -> 85.8 us
    all_gather x1 -> x0, waiting for transfers between devices: 72.4 us -> none  [local(): lax.all_gather(upper_right, 'dp', axis=1, tiled=True)]
    all_gather x1, waiting for transfers between devices: 97.4 us -> 71 us  [local(): lax.all_gather(lower_right, 'dp', axis=1, tiled=True)]
    all_to_all x0 -> x1, starting transfers between devices: none -> 12.6 us  [lax.all_to_all(jnp.stack(lax.axis_size('dp') * [view], axis=0), 'dp', 0, 0)]
  transfers between devices with their start and end apart: 12 -> 12, of which waited for: 11 -> 10; matrix products, arithmetic and copies ran while one was open for 4% -> 5% of each run, Pallas kernels for 0% -> 0%
where the time goes in v1:
time: 850 us; the launch traced here: 849 us
  waiting for transfers between devices  695 us (82%)
  starting transfers between devices  85.8 us (10%)
  local copies, waits for them, and re-layouts  25.4 us (3%)
  matrix products  22.2 us (3%)
  between operations  14.3 us (2%)
    reduce_scatter x1, waiting for transfers between devices, local(): lax.psum_scatter(grad_lower_right.astype(jnp.bfloat16), 'dp', scatter_dim...  105 us
    reduce_scatter x1, waiting for transfers between devices, local(): lax.psum_scatter(grad_lower_left.astype(jnp.bfloat16), 'dp', scatter_dime...  102 us
    all_gather x1, waiting for transfers between devices, local(): lax.all_gather(lower_left, 'dp', axis=1, tiled=True)  101 us
    all_gather x1, waiting for transfers between devices, local(): lax.all_gather(upper_left, 'dp', axis=1, tiled=True)  99.6 us
    reduce_scatter x1, waiting for transfers between devices, local(): lax.psum_scatter(grad_upper_left.astype(jnp.bfloat16), 'dp', scatter_dime...  97.9 us
    all_to_all x4, waiting for transfers between devices, permute(): lax.all_to_all(values, 'block', split_axis=1, concat_axis=0, tiled=True)  76.8 us
    all_to_all x4, starting transfers between devices, permute(): lax.all_to_all(values, 'block', split_axis=1, concat_axis=0, tiled=True)  72.7 us
    all_gather x1, waiting for transfers between devices, local(): lax.all_gather(lower_right, 'dp', axis=1, tiled=True)  71 us
  transfers between devices with their start and end apart: 12, of which 10 were waited for; matrix products, arithmetic and copies ran while one was open for 5% of the time, Pallas kernels for 0%

profile of v1, /device:TPU:6, one launch (start us, length us, event | category | flops | bytes accessed | tf_op | source)
XLA Modules:
  0.0 848.9 jit_solution(16480845466362094097)
XLA Ops:
  7.2 2.0 stack.2
  9.2 12.6 %all-to-all-start.1 = ((bf16[16,8,16,256]{3,2,1,0:T(8,128)(2,1)}), bf16[16,8,16,256]{3,2,1,0:T(8,128)(2,1)S(1)}, u32[]{:S(2)}, u32[]{:S(2)}) async-start(bf16[16,8,16,256]{3,2,1,0:T(8,128)(2,1)} %stack.2), calls=%async_computation.1 | async-start | bytes 2097152 | tf_op jit(solution)/shard_map/all_to_all | solution.py:7
  21.8 0.0 all-gather.4.cloned.1.call-start
  21.9 0.7 all-gather.4.cloned.1.call-update
  22.6 0.1 reshape.60
  22.6 99.6 %all-gather.4.cloned.1.call-done = bf16[2,256,1024]{2,1,0:T(8,128)(2,1)} async-done(((bf16[2,16,1024]{2,1,0:T(8,128)(2,1)}), bf16[2,256,1024]{2,1,0:T(8,128)(2,1)}) %all-gather.4.cloned.1.call-update) | async-done | bytes 1048592 | tf_op jit(solution)/shard_map/all_gather | solution.py:49
  122.3 1.5 copy.72
  123.8 0.5 convolution_convert_fusion.7
  124.2 1.5 copy.74
  125.8 18.9 %all-to-all-start = ((bf16[8,256,256]{2,0,1:T(8,128)(2,1)}), bf16[8,256,256]{2,0,1:T(8,128)(2,1)S(1)}, u32[]{:S(2)}, u32[]{:S(2)}) async-start(bf16[8,256,256]{2,0,1:T(8,128)(2,1)} %copy.74), calls=%async_computation | async-start | bytes 2097152 | tf_op jit(solution)/shard_map/all_to_all | solution.py:16
  144.7 0.0 all-gather.8.cloned.1.call-start
  144.7 0.7 all-gather.8.cloned.1.call-update
  145.4 1.7 reshape.67
  147.2 100.8 %all-gather.8.cloned.1.call-done = bf16[2,1024,256]{2,1,0:T(8,128)(2,1)} async-done(((bf16[2,64,256]{2,1,0:T(8,128)(2,1)}), bf16[2,1024,256]{2,1,0:T(8,128)(2,1)}) %all-gather.8.cloned.1.call-update) | async-done | bytes 1048592 | tf_op jit(solution)/shard_map/all_gather | solution.py:52
  248.0 1.7 convolution_convert_fusion.5
  249.7 1.5 copy.84
  251.2 16.9 %all-to-all-start.3 = ((bf16[8,256,256]{2,0,1:T(8,128)(2,1)}), bf16[8,256,256]{2,0,1:T(8,128)(2,1)}, u32[]{:S(2)}, u32[]{:S(2)}) async-start(bf16[8,256,256]{2,0,1:T(8,128)(2,1)} %copy.84), calls=%async_computation.3 | async-start | bytes 2097152 | tf_op jit(solution)/shard_map/all_to_all | solution.py:16
  268.2 0.0 all-gather.6.cloned.1.call-start
  268.2 0.7 all-gather.6.cloned.1.call-update
  268.9 0.1 copy.77
  269.0 1.1 copy-done.4
  270.1 0.3 copy.76
  270.4 25.6 %all-to-all-done.3 = bf16[8,256,256]{2,0,1:T(8,128)(2,1)} async-done(((bf16[8,256,256]{2,0,1:T(8,128)(2,1)}), bf16[8,256,256]{2,0,1:T(8,128)(2,1)}, u32[]{:S(2)}, u32[]{:S(2)}) %all-to-all-start.3) | async-done | bytes 1048608 | tf_op jit(solution)/shard_map/all_to_all | solution.py:16
  296.0 2.5 copy.86
  298.5 1.8 fusion.17
  300.4 71.0 %all-gather.6.cloned.1.call-done = bf16[8,256,256]{2,1,0:T(8,128)(2,1)} async-done(((bf16[8,16,256]{2,1,0:T(8,128)(2,1)}), bf16[8,256,256]{2,1,0:T(8,128)(2,1)}) %all-gather.6.cloned.1.call-update) | async-done | bytes 1048592 | tf_op jit(solution)/shard_map/all_gather | solution.py:51
  371.4 3.9 fusion.6
  375.4 0.9 copy-done
  376.3 1.4 fusion.12
  377.8 2.7 copy.88
  380.5 16.2 %all-to-all-start.4 = ((bf16[8,256,256]{2,0,1:T(8,128)(2,1)}), bf16[8,256,256]{2,0,1:T(8,128)(2,1)}, u32[]{:S(2)}, u32[]{:S(2)}) async-start(bf16[8,256,256]{2,0,1:T(8,128)(2,1)} %copy.88), calls=%async_computation.4 | async-start | bytes 2097152 | tf_op jit(solution)/shard_map/all_to_all | solution.py:16
  396.7 0.0 reduce-scatter.7.cloned.1.call-start
  396.8 1.4 convolution_convert_fusion.2
  398.2 0.0 reduce-scatter.7.cloned.1.call-update
  398.2 2.7 fusion.11
  400.9 1.9 copy.79
  402.7 26.2 %all-to-all-done.4 = bf16[8,256,256]{2,0,1:T(8,128)(2,1)} async-done(((bf16[8,256,256]{2,0,1:T(8,128)(2,1)}), bf16[8,256,256]{2,0,1:T(8,128)(2,1)}, u32[]{:S(2)}, u32[]{:S(2)}) %all-to-all-start.4) | async-done | bytes 1048608 | tf_op jit(solution)/shard_map/all_to_all | solution.py:16
  428.9 20.7 %all-to-all-start.2 = ((bf16[8,256,256]{2,0,1:T(8,128)(2,1)}), bf16[8,256,256]{2,0,1:T(8,128)(2,1)S(1)}, u32[]{:S(2)}, u32[]{:S(2)}) async-start(bf16[8,256,256]{2,0,1:T(8,128)(2,1)} %copy.79), calls=%async_computation.2 | async-start | bytes 2097152 | tf_op jit(solution)/shard_map/all_to_all | solution.py:16
  449.6 0.0 reduce-scatter.9.cloned.1.call-start
  449.7 3.7 convolution_convert_fusion.1
  453.3 0.0 reduce-scatter.9.cloned.1.call-update
  453.4 0.2 reduce-scatter.5.cloned.1.call-start
  453.6 1.3 copy.90
  454.9 1.4 convolution_convert_fusion.3
  456.3 2.3 copy.93
  458.5 0.0 reduce-scatter.5.cloned.1.call-update
  458.6 0.0 reduce-scatter.11.cloned.1.call-start
  458.6 25.0 %all-to-all-done.2 = bf16[8,256,256]{2,0,1:T(8,128)(2,1)S(1)} async-done(((bf16[8,256,256]{2,0,1:T(8,128)(2,1)}), bf16[8,256,256]{2,0,1:T(8,128)(2,1)S(1)}, u32[]{:S(2)}, u32[]{:S(2)}) %all-to-all-start.2) | async-done | bytes 1048608 | tf_op jit(solution)/shard_map/all_to_all | solution.py:16
  483.6 0.9 copy-done.2
  484.6 1.3 copy.81
  485.9 1.4 convolution_convert_fusion
  487.3 0.0 reduce-scatter.11.cloned.1.call-update
  487.3 39.6 %reduce-scatter.7.cloned.1.call-done = bf16[8,16,256]{2,1,0:T(8,128)(2,1)} async-done(((bf16[8,256,256]{2,1,0:T(8,128)(2,1)}), bf16[8,16,256]{2,1,0:T(8,128)(2,1)}) %reduce-scatter.7.cloned.1.call-update) | async-done | bytes 65552 | tf_op jit(solution)/shard_map/reduce_scatter | solution.py:91
  526.9 1.5 convert_element_type.89
  528.4 105.1 %reduce-scatter.9.cloned.1.call-done = bf16[8,16,256]{2,1,0:T(8,128)(2,1)} async-done(((bf16[8,256,256]{2,1,0:T(8,128)(2,1)}), bf16[8,16,256]{2,1,0:T(8,128)(2,1)}) %reduce-scatter.9.cloned.1.call-update) | async-done | bytes 65552 | tf_op jit(solution)/shard_map/reduce_scatter | solution.py:94
  633.5 1.5 convert_element_type.91
  635.0 1.7 fusion.13
  636.7 0.8 copy.99
  637.6 0.5 fusion.14
  638.1 0.8 copy.100
  639.0 97.9 %reduce-scatter.5.cloned.1.call-done = bf16[2,16,1024]{2,1,0:T(8,128)(2,1)} async-done(((bf16[2,256,1024]{2,1,0:T(8,128)(2,1)}), bf16[2,16,1024]{2,1,0:T(8,128)(2,1)}) %reduce-scatter.5.cloned.1.call-update) | async-done | bytes 65552 | tf_op jit(solution)/shard_map/reduce_scatter | solution.py:88
  736.9 1.5 convert_element_type.87
  738.4 102.1 %reduce-scatter.11.cloned.1.call-done = bf16[2,64,256]{2,1,0:T(8,128)(2,1)} async-done(((bf16[2,1024,256]{2,1,0:T(8,128)(2,1)}), bf16[2,64,256]{2,1,0:T(8,128)(2,1)}) %reduce-scatter.11.cloned.1.call-update) | async-done | bytes 65552 | tf_op jit(solution)/shard_map/reduce_scatter | solution.py:97
  840.5 1.5 convert_element_type.95
  (15 shorter events, 0.0 us)
Async XLA Ops:
  7.2 15.4 %copy-start.7 = (bf16[256,512]{1,0:T(8,128)(2,1)S(1)}, bf16[256,512]{1,0:T(8,128)(2,1)}, u32[]{:S(2)}) copy-start(bf16[256,512]{1,0:T(8,128)(2,1)} %param.6) | copy-start | bytes 786436
  9.2 116.6 %all-to-all-start.1 = ((bf16[16,8,16,256]{3,2,1,0:T(8,128)(2,1)}), bf16[16,8,16,256]{3,2,1,0:T(8,128)(2,1)S(1)}, u32[]{:S(2)}, u32[]{:S(2)}) async-start(bf16[16,8,16,256]{3,2,1,0:T(8,128)(2,1)} %stack.2), calls=%async_computation.1 | async-start | bytes 2097152 | tf_op jit(solution)/shard_map/all_to_all | solution.py:7
  21.8 100.5 %all-gather.4.cloned.1.call-start = ((), (), s32[]{:S(2)}) async-start(), calls=%async_computation.9 | async-start | bytes 1114112 | tf_op jit(solution)/shard_map/all_gather | solution.py:49
  125.8 125.5 %all-to-all-start = ((bf16[8,256,256]{2,0,1:T(8,128)(2,1)}), bf16[8,256,256]{2,0,1:T(8,128)(2,1)S(1)}, u32[]{:S(2)}, u32[]{:S(2)}) async-start(bf16[8,256,256]{2,0,1:T(8,128)(2,1)} %copy.74), calls=%async_computation | async-start | bytes 2097152 | tf_op jit(solution)/shard_map/all_to_all | solution.py:16
  144.7 103.3 %all-gather.8.cloned.1.call-start = ((), (), s32[]{:S(2)}) async-start(), calls=%async_computation.11 | async-start | bytes 1114112 | tf_op jit(solution)/shard_map/all_gather | solution.py:52
  251.2 17.7 %copy-start.3 = (bf16[8,256,256]{2,0,1:T(8,128)(2,1)}, bf16[8,256,256]{2,0,1:T(8,128)(2,1)S(1)}, u32[]{:S(2)}) copy-start(bf16[8,256,256]{2,0,1:T(8,128)(2,1)S(1)} %all-to-all-done) | copy-start | bytes 3145732
  251.2 44.8 %all-to-all-start.3 = ((bf16[8,256,256]{2,0,1:T(8,128)(2,1)}), bf16[8,256,256]{2,0,1:T(8,128)(2,1)}, u32[]{:S(2)}, u32[]{:S(2)}) async-start(bf16[8,256,256]{2,0,1:T(8,128)(2,1)} %copy.84), calls=%async_computation.3 | async-start | bytes 2097152 | tf_op jit(solution)/shard_map/all_to_all | solution.py:16
  268.2 103.3 %all-gather.6.cloned.1.call-start = ((), (), s32[]{:S(2)}) async-start(), calls=%async_computation.10 | async-start | bytes 1114112 | tf_op jit(solution)/shard_map/all_gather | solution.py:51
  268.9 1.2 copy-start.4
  375.4 1.0 copy-start
  377.8 19.0 %copy-start.1 = (bf16[8,256,256]{1,2,0:T(8,128)(2,1)S(1)}, bf16[8,256,256]{1,2,0:T(8,128)(2,1)}, u32[]{:S(2)}) copy-start(bf16[8,256,256]{1,2,0:T(8,128)(2,1)} %copy-done) | copy-start | bytes 3145732
  380.5 48.4 %all-to-all-start.4 = ((bf16[8,256,256]{2,0,1:T(8,128)(2,1)}), bf16[8,256,256]{2,0,1:T(8,128)(2,1)}, u32[]{:S(2)}, u32[]{:S(2)}) async-start(bf16[8,256,256]{2,0,1:T(8,128)(2,1)} %copy.88), calls=%async_computation.4 | async-start | bytes 2097152 | tf_op jit(solution)/shard_map/all_to_all | solution.py:16
  396.7 130.2 %reduce-scatter.7.cloned.1.call-start = ((), (), s32[]{:S(2)}) async-start(), calls=%async_computation.13 | async-start | bytes 1114112 | tf_op jit(solution)/shard_map/reduce_scatter | solution.py:91
  400.9 48.8 %copy-start.6 = (bf16[32,8,8,256]{3,2,1,0:T(8,128)(2,1)S(1)}, bf16[32,8,8,256]{3,2,1,0:T(8,128)(2,1)}, u32[]{:S(2)}) copy-start(bf16[32,8,8,256]{3,2,1,0:T(8,128)(2,1)} %copy.86) | copy-start | bytes 3145732
  428.9 54.8 %all-to-all-start.2 = ((bf16[8,256,256]{2,0,1:T(8,128)(2,1)}), bf16[8,256,256]{2,0,1:T(8,128)(2,1)S(1)}, u32[]{:S(2)}, u32[]{:S(2)}) async-start(bf16[8,256,256]{2,0,1:T(8,128)(2,1)} %copy.79), calls=%async_computation.2 | async-start | bytes 2097152 | tf_op jit(solution)/shard_map/all_to_all | solution.py:16
  449.6 183.9 %reduce-scatter.9.cloned.1.call-start = ((), (), s32[]{:S(2)}) async-start(), calls=%async_computation.14 | async-start | bytes 1114112 | tf_op jit(solution)/shard_map/reduce_scatter | solution.py:94
  453.4 283.5 %reduce-scatter.5.cloned.1.call-start = ((), (), s32[]{:S(2)}) async-start(), calls=%async_computation.12 | async-start | bytes 1114112 | tf_op jit(solution)/shard_map/reduce_scatter | solution.py:88
  458.5 27.3 %copy-start.5 = (bf16[256,2,256]{2,1,0:T(2,128)(2,1)S(1)}, bf16[256,2,256]{2,1,0:T(2,128)(2,1)}, u32[]{:S(2)}) copy-start(bf16[256,2,256]{2,1,0:T(2,128)(2,1)} %reshape.67) | copy-start | bytes 786436
  458.6 382.0 %reduce-scatter.11.cloned.1.call-start = ((), (), s32[]{:S(2)}) async-start(), calls=%async_computation.15 | async-start | bytes 1114112 | tf_op jit(solution)/shard_map/reduce_scatter | solution.py:97
  483.6 0.9 copy-start.2
Sparse Core Ops, SparseCore 0:
  24.7 97.5 all-gather.3
  147.6 100.3 all-gather.7
  271.1 100.3 all-gather.5
  400.0 126.8 reduce-scatter.6
  529.6 103.8 reduce-scatter.8
  636.1 100.7 reduce-scatter.4
  739.7 100.7 reduce-scatter.10
